TPU v7x, 32 devices: a whole 2x2x4 slice. The times are simulated.
32 devices in a mesh: blk: 32 (over z, y, x, core).
Axes of the slice: x: 2, y: 2, z: 4, core: 2. Of those that a mesh axis runs over, the one named last changes fastest.
Arguments:
- samples: bfloat16 [8192, 2048], P('blk'), may hold values from -6 to 6
- hubs: int32 [64], replicated, may hold values from 0 to 8191, as said below
- start: int32 [1], replicated, may hold values from 1 to 13
Outputs:
- self_stat: float32 [8192, 256], P('blk')
- ahead_stat: float32 [3, 8192, 256], P(None, 'blk')
- behind_stat: float32 [3, 8192, 256], P(None, 'blk')
Inputs may be any that keep to these rules, and one draw needn't show every extreme that they name: `hubs`: the 64 indices are distinct.
All inputs are finite; a program needn't handle non-finite values.
Results may differ from a plain program's by a relative error of at most 0.0049.
Values may be sent and summed in bfloat16 or wider, within the bound.
No kernel may reach another device: no remote copies, remote signals or barrier semaphores. Data moves between devices by JAX's collectives and lax.ppermute only.
A program may use at most 64 MiB of HBM per device.

v0:
```python
import math
import jax
import jax.numpy as jnp
from jax import lax
from jax.sharding import PartitionSpec as P


def shifted(block, axis, distance):
    devices = range(lax.axis_size(axis))
    route = [((i - distance) % len(devices), i) for i in devices]
    return lax.ppermute(block, axis, route)


def row_scale(resid):
    wide = resid.astype(jnp.float32)
    return 1.0 / jnp.sqrt(jnp.maximum(jnp.sum(wide * wide, axis=1), 1.0))


def correlate(resid, scale, partner):
    dots = lax.dot_general(
        resid, partner, (((1,), (1,)), ((), ())), preferred_element_type=jnp.float32
    )
    return (dots * scale[:, None] * row_scale(partner)[None, :]).astype(jnp.bfloat16)


def to_stat(rounded, factor):
    values = lax.optimization_barrier(rounded).astype(jnp.float32)
    return factor * (0.5 * (jnp.log1p(values) - jnp.log1p(-values)))


def shards(samples, hubs, start):
    rows = samples.shape[0]
    width = samples.shape[1]
    factor = math.sqrt(width - hubs.shape[0] - 3)
    count = lax.axis_size("blk")
    mine = lax.axis_index("blk")
    levels = count.bit_length() - 2
    offset = start[0]
    owner = hubs // rows
    within = hubs % rows
    picker = jnp.logical_and(
        (owner == mine)[:, None], within[:, None] == jnp.arange(rows, dtype=jnp.int32)[None, :]
    ).astype(jnp.bfloat16)
    hub_rows = lax.psum(jnp.dot(picker, samples, preferred_element_type=jnp.float32), "blk")
    gram = jnp.dot(hub_rows, hub_rows.T, precision=lax.Precision.HIGHEST)
    proj = jnp.dot(samples, hub_rows.astype(jnp.bfloat16).T, preferred_element_type=jnp.float32)
    factor_lower = jnp.linalg.cholesky(gram)
    coef = jax.scipy.linalg.cho_solve((factor_lower, True), proj.T).T
    resid = (
        samples.astype(jnp.float32) - jnp.dot(coef, hub_rows, precision=lax.Precision.HIGHEST)
    ).astype(jnp.bfloat16)
    scale = row_scale(resid)
    own = correlate(resid, scale, resid)
    diag = jnp.arange(rows)[:, None] == jnp.arange(rows)[None, :]
    own_stat = jnp.where(diag, 0.0, to_stat(own, factor))
    partner = resid
    for level in range(levels):
        moved = shifted(partner, "blk", -(1 << level))
        partner = jnp.where(offset >> level & 1 == 1, moved, partner)
    ahead = []
    turned = []
    for index in range(3):
        if index > 0:
            partner = shifted(partner, "blk", -1)
        tile = correlate(resid, scale, partner)
        ahead.append(to_stat(tile, factor))
        turned.append(tile.T)
    returned = []
    for index in range(3):
        tile = turned[index]
        for extra in range(index):
            tile = shifted(tile, "blk", 1)
        for level in range(levels):
            moved = shifted(tile, "blk", 1 << level)
            tile = jnp.where(offset >> level & 1 == 1, moved, tile)
        returned.append(tile)
    behind = jnp.stack([to_stat(tile, factor) for tile in returned])
    return (own_stat, jnp.stack(ahead), behind)


def solution(mesh):
    in_specs = (P("blk", None), P(), P())
    out_specs = (P("blk", None), P(None, "blk", None), P(None, "blk", None))
    return jax.shard_map(shards, mesh=mesh, in_specs=in_specs, out_specs=out_specs, check_vma=False)
```

profile of v0, /device:TPU:0, one launch (start us, length us, event | category | flops | bytes accessed | tf_op | source)
XLA Modules:
  0.0 362.8 jit_solution(15652582608777804637)
XLA Ops:
  7.2 0.7 and_select_fusion
  7.9 0.7 fusion.50
  8.5 2.4 fusion.40
  10.9 134.7 %all-reduce.2.cloned.1.call-done = f32[64,2048]{1,0:T(8,128)} async-done(((f32[64,2048]{1,0:T(8,128)}), f32[64,2048]{1,0:T(8,128)}) %all-reduce.2.cloned.1.call-update) | async-done | bytes 524304 | tf_op jit(solution)/shard_map/psum | solution.py:44
  145.6 1.8 fusion.51
  147.5 0.1 copy.6
  147.6 5.8 %cholesky.16 = f32[64,64]{1,0:T(8,128)S(1)} custom-call(f32[64,64]{1,0:T(8,128)S(1)} %fusion.47), custom_call_target="Cholesky" | custom-call | tf_op jit(solution)/shard_map/jit(cholesky)/cholesky | solution.py:47
  153.4 0.6 compare_reduce_fusion
  154.1 0.7 fusion.42
  154.7 4.9 %custom-call.10 = f32[1,64,64]{1,2,0:T(8,128)S(1)} custom-call(f32[1,64,64]{2,1,0:T(8,128)S(1)} %fusion.42), custom_call_target="InvertDiagBlocksLowerTriangular" | custom-call | tf_op jit(solution)/shard_map/jit(_cho_solve)/triangular_solve | solution.py:48
  159.7 0.4 fusion.37
  160.1 0.3 fusion.45
  160.4 0.2 fusion.43
  160.6 2.1 multiply_reduce_fusion.3
  162.6 1.9 collective-permute-start
  165.2 11.7 %collective-permute-done = bf16[256,2048]{1,0:T(8,128)(2,1)S(1)} collective-permute-done((bf16[256,2048]{1,0:T(8,128)(2,1)S(1)}, bf16[256,2048]{1,0:T(8,128)(2,1)S(1)}, u32[]{:S(2)}, u32[]{:S(2)}) %collective-permute-start) | collective-permute-done | bytes 1048608 | tf_op jit(solution)/shard_map/ppermute | solution.py:11
  176.9 0.1 broadcast_select_fusion
  177.0 1.4 collective-permute-start.1
  178.4 23.6 %collective-permute-done.1 = bf16[256,2048]{1,0:T(8,128)(2,1)S(1)} collective-permute-done((bf16[256,2048]{1,0:T(8,128)(2,1)S(1)}, bf16[256,2048]{1,0:T(8,128)(2,1)S(1)}, u32[]{:S(2)}, u32[]{:S(2)}) %collective-permute-start.1) | collective-permute-done | bytes 1048608 | tf_op jit(solution)/shard_map/ppermute | solution.py:11
  202.0 0.1 broadcast_select_fusion.1
  202.1 0.8 collective-permute-start.2
  202.9 24.4 %collective-permute-done.2 = bf16[256,2048]{1,0:T(8,128)(2,1)S(1)} collective-permute-done((bf16[256,2048]{1,0:T(8,128)(2,1)S(1)}, bf16[256,2048]{1,0:T(8,128)(2,1)S(1)}, u32[]{:S(2)}, u32[]{:S(2)}) %collective-permute-start.2) | collective-permute-done | bytes 1048608 | tf_op jit(solution)/shard_map/ppermute | solution.py:11
  227.3 0.1 broadcast_select_fusion.2
  227.4 1.5 collective-permute-start.3
  229.0 22.8 %collective-permute-done.3 = bf16[256,2048]{1,0:T(8,128)(2,1)S(1)} collective-permute-done((bf16[256,2048]{1,0:T(8,128)(2,1)S(1)}, bf16[256,2048]{1,0:T(8,128)(2,1)S(1)}, u32[]{:S(2)}, u32[]{:S(2)}) %collective-permute-start.3) | collective-permute-done | bytes 1048608 | tf_op jit(solution)/shard_map/ppermute | solution.py:11
  251.8 0.5 multiply_reduce_fusion.2
  252.3 6.7 %collective-permute-start.4 = (bf16[256,2048]{1,0:T(8,128)(2,1)S(1)}, bf16[256,2048]{1,0:T(8,128)(2,1)S(1)}, u32[]{:S(2)}, u32[]{:S(2)}) collective-permute-start(bf16[256,2048]{1,0:T(8,128)(2,1)S(1)} %get-tuple-element.7), channel_id=1, source_target_pairs={{1,0},{2,1},{3,2},{4,3},{5,4},{6,5},{7,6},{8,7},{9,8},{10,9},{11,1... | collective-permute-start | bytes 3145736 | tf_op jit(solution)/shard_map/ppermute | solution.py:11
  259.0 0.5 fusion.6
  259.4 0.1 collective-permute-start.6
  259.5 0.5 fusion.5
  260.0 7.6 %collective-permute-done.6 = bf16[256,256]{1,0:T(8,128)(2,1)S(1)} collective-permute-done((bf16[256,256]{1,0:T(8,128)(2,1)S(1)}, bf16[256,256]{1,0:T(8,128)(2,1)S(1)}, u32[]{:S(2)}, u32[]{:S(2)}) %collective-permute-start.6) | collective-permute-done | bytes 131104 | tf_op jit(solution)/shard_map/ppermute | solution.py:11
  267.6 0.1 collective-permute-start.7
  267.7 0.9 fusion.11
  268.6 7.6 %collective-permute-done.7 = bf16[256,256]{1,0:T(8,128)(2,1)S(1)} collective-permute-done((bf16[256,256]{1,0:T(8,128)(2,1)S(1)}, bf16[256,256]{1,0:T(8,128)(2,1)S(1)}, u32[]{:S(2)}, u32[]{:S(2)}) %collective-permute-start.7) | collective-permute-done | bytes 131104 | tf_op jit(solution)/shard_map/ppermute | solution.py:11
  276.3 0.3 multiply_reduce_fusion.1
  276.6 0.6 fusion.7
  277.2 0.1 collective-permute-start.10
  277.3 5.3 %collective-permute-start.5 = (bf16[256,2048]{1,0:T(8,128)(2,1)S(1)}, bf16[256,2048]{1,0:T(8,128)(2,1)S(1)}, u32[]{:S(2)}, u32[]{:S(2)}) collective-permute-start(bf16[256,2048]{1,0:T(8,128)(2,1)S(1)} %collective-permute-done.4), channel_id=1, source_target_pairs={{1,0},{2,1},{3,2},{4,3},{5,4},{6,5},{7,6},{8,7},{9,8},{10,9},{11,1... | collective-permute-start | bytes 3145736 | tf_op jit(solution)/shard_map/ppermute | solution.py:11
  282.6 0.2 fusion.15
  282.8 2.6 collective-permute-done.10
  285.4 0.1 collective-permute-start.9
  285.5 8.0 %collective-permute-done.11 = bf16[256,256]{1,0:T(8,128)(2,1)S(1)} collective-permute-done((bf16[256,256]{1,0:T(8,128)(2,1)S(1)}, bf16[256,256]{1,0:T(8,128)(2,1)S(1)}, u32[]{:S(2)}, u32[]{:S(2)}) %collective-permute-start.11) | collective-permute-done | bytes 131104 | tf_op jit(solution)/shard_map/ppermute | solution.py:11
  293.5 0.1 collective-permute-start.12
  293.5 4.7 %collective-permute-done.9 = bf16[256,256]{1,0:T(8,128)(2,1)S(1)} collective-permute-done((bf16[256,256]{1,0:T(8,128)(2,1)S(1)}, bf16[256,256]{1,0:T(8,128)(2,1)S(1)}, u32[]{:S(2)}, u32[]{:S(2)}) %collective-permute-start.9) | collective-permute-done | bytes 131104 | tf_op jit(solution)/shard_map/ppermute | solution.py:11
  298.3 5.6 %collective-permute-done.12 = bf16[256,256]{1,0:T(8,128)(2,1)S(1)} collective-permute-done((bf16[256,256]{1,0:T(8,128)(2,1)S(1)}, bf16[256,256]{1,0:T(8,128)(2,1)S(1)}, u32[]{:S(2)}, u32[]{:S(2)}) %collective-permute-start.12) | collective-permute-done | bytes 131104 | tf_op jit(solution)/shard_map/ppermute | solution.py:11
  303.9 0.1 collective-permute-start.13
  304.0 0.3 multiply_reduce_fusion
  304.2 0.6 fusion.8
  304.9 6.8 %collective-permute-done.13 = bf16[256,256]{1,0:T(8,128)(2,1)S(1)} collective-permute-done((bf16[256,256]{1,0:T(8,128)(2,1)S(1)}, bf16[256,256]{1,0:T(8,128)(2,1)S(1)}, u32[]{:S(2)}, u32[]{:S(2)}) %collective-permute-start.13) | collective-permute-done | bytes 131104 | tf_op jit(solution)/shard_map/ppermute | solution.py:11
  311.7 0.1 collective-permute-start.14
  311.7 2.5 collective-permute-done.15
  314.2 0.2 fusion.19
  314.4 7.8 %collective-permute-done.16 = bf16[256,256]{1,0:T(8,128)(2,1)S(1)} collective-permute-done((bf16[256,256]{1,0:T(8,128)(2,1)S(1)}, bf16[256,256]{1,0:T(8,128)(2,1)S(1)}, u32[]{:S(2)}, u32[]{:S(2)}) %collective-permute-start.16) | collective-permute-done | bytes 131104 | tf_op jit(solution)/shard_map/ppermute | solution.py:11
  322.3 8.0 %collective-permute-done.17 = bf16[256,256]{1,0:T(8,128)(2,1)S(1)} collective-permute-done((bf16[256,256]{1,0:T(8,128)(2,1)S(1)}, bf16[256,256]{1,0:T(8,128)(2,1)S(1)}, u32[]{:S(2)}, u32[]{:S(2)}) %collective-permute-start.17) | collective-permute-done | bytes 131104 | tf_op jit(solution)/shard_map/ppermute | solution.py:11
  330.2 0.1 collective-permute-start.18
  330.3 0.4 fusion.27
  330.7 9.5 %collective-permute-done.18 = bf16[256,256]{1,0:T(8,128)(2,1)S(1)} collective-permute-done((bf16[256,256]{1,0:T(8,128)(2,1)S(1)}, bf16[256,256]{1,0:T(8,128)(2,1)S(1)}, u32[]{:S(2)}, u32[]{:S(2)}) %collective-permute-start.18) | collective-permute-done | bytes 131104 | tf_op jit(solution)/shard_map/ppermute | solution.py:11
  340.3 0.2 fusion.23
  340.5 7.5 %collective-permute-done.19 = bf16[256,256]{1,0:T(8,128)(2,1)S(1)} collective-permute-done((bf16[256,256]{1,0:T(8,128)(2,1)S(1)}, bf16[256,256]{1,0:T(8,128)(2,1)S(1)}, u32[]{:S(2)}, u32[]{:S(2)}) %collective-permute-start.19) | collective-permute-done | bytes 131104 | tf_op jit(solution)/shard_map/ppermute | solution.py:11
  348.0 0.1 collective-permute-start.20
  348.1 1.1 copy.14
  349.3 5.5 %collective-permute-done.20 = bf16[256,256]{1,0:T(8,128)(2,1)S(1)} collective-permute-done((bf16[256,256]{1,0:T(8,128)(2,1)S(1)}, bf16[256,256]{1,0:T(8,128)(2,1)S(1)}, u32[]{:S(2)}, u32[]{:S(2)}) %collective-permute-start.20) | collective-permute-done | bytes 131104 | tf_op jit(solution)/shard_map/ppermute | solution.py:11
  354.8 0.2 fusion.35
  355.0 0.9 pad_maximum_fusion.1
  (35 shorter events, 0.6 us)
Async XLA Ops:
  7.2 138.5 %all-reduce.2.cloned.1.call-start = ((), (), s32[]{:S(2)}) async-start(), calls=%async_computation | async-start | bytes 1048576 | tf_op jit(solution)/shard_map/psum | solution.py:44
  10.9 148.7 %copy-start = (bf16[256,2048]{1,0:T(8,128)(2,1)S(1)}, bf16[256,2048]{1,0:T(8,128)(2,1)}, u32[]{:S(2)}) copy-start(bf16[256,2048]{1,0:T(8,128)(2,1)} %param.3) | copy-start | bytes 3145732
  145.6 14.0 %copy-start.1 = (f32[64,2048]{1,0:T(8,128)S(1)}, f32[64,2048]{1,0:T(8,128)}, u32[]{:S(2)}) copy-start(f32[64,2048]{1,0:T(8,128)} %all-reduce.2.cloned.1.call-done) | copy-start | bytes 1572868
  162.6 14.2 %collective-permute-start = (bf16[256,2048]{1,0:T(8,128)(2,1)S(1)}, bf16[256,2048]{1,0:T(8,128)(2,1)S(1)}, u32[]{:S(2)}, u32[]{:S(2)}) collective-permute-start(bf16[256,2048]{1,0:T(8,128)(2,1)S(1)} %get-tuple-element.9), channel_id=1, source_target_pairs={{1,0},{2,1},{3,2},{4,3},{5,4},{6,5},{7,6},{8,7},{9,8},{10,9},{11,1... | collective-permute-start | bytes 3145736 | tf_op jit(solution)/shard_map/ppermute | solution.py:11
  177.0 25.0 %collective-permute-start.1 = (bf16[256,2048]{1,0:T(8,128)(2,1)S(1)}, bf16[256,2048]{1,0:T(8,128)(2,1)S(1)}, u32[]{:S(2)}, u32[]{:S(2)}) collective-permute-start(bf16[256,2048]{1,0:T(8,128)(2,1)S(1)} %broadcast_select_fusion), channel_id=1, source_target_pairs={{2,0},{3,1},{4,2},{5,3},{6,4},{7,5},{8,6},{9,7},{10,8},{11,9},{12,... | collective-permute-start | bytes 3145736 | tf_op jit(solution)/shard_map/ppermute | solution.py:11
  202.1 25.2 %collective-permute-start.2 = (bf16[256,2048]{1,0:T(8,128)(2,1)S(1)}, bf16[256,2048]{1,0:T(8,128)(2,1)S(1)}, u32[]{:S(2)}, u32[]{:S(2)}) collective-permute-start(bf16[256,2048]{1,0:T(8,128)(2,1)S(1)} %broadcast_select_fusion.1), channel_id=1, source_target_pairs={{4,0},{5,1},{6,2},{7,3},{8,4},{9,5},{10,6},{11,7},{12,8},{13,9},{1... | collective-permute-start | bytes 3145736 | tf_op jit(solution)/shard_map/ppermute | solution.py:11
  227.4 24.4 %collective-permute-start.3 = (bf16[256,2048]{1,0:T(8,128)(2,1)S(1)}, bf16[256,2048]{1,0:T(8,128)(2,1)S(1)}, u32[]{:S(2)}, u32[]{:S(2)}) collective-permute-start(bf16[256,2048]{1,0:T(8,128)(2,1)S(1)} %broadcast_select_fusion.2), channel_id=1, source_target_pairs={{8,0},{9,1},{10,2},{11,3},{12,4},{13,5},{14,6},{15,7},{16,8},{17,9... | collective-permute-start | bytes 3145736 | tf_op jit(solution)/shard_map/ppermute | solution.py:11
  252.3 24.0 %collective-permute-start.4 = (bf16[256,2048]{1,0:T(8,128)(2,1)S(1)}, bf16[256,2048]{1,0:T(8,128)(2,1)S(1)}, u32[]{:S(2)}, u32[]{:S(2)}) collective-permute-start(bf16[256,2048]{1,0:T(8,128)(2,1)S(1)} %get-tuple-element.7), channel_id=1, source_target_pairs={{1,0},{2,1},{3,2},{4,3},{5,4},{6,5},{7,6},{8,7},{9,8},{10,9},{11,1... | collective-permute-start | bytes 3145736 | tf_op jit(solution)/shard_map/ppermute | solution.py:11
  259.4 8.1 %collective-permute-start.6 = (bf16[256,256]{1,0:T(8,128)(2,1)S(1)}, bf16[256,256]{1,0:T(8,128)(2,1)S(1)}, u32[]{:S(2)}, u32[]{:S(2)}) collective-permute-start(bf16[256,256]{1,0:T(8,128)(2,1)S(1)} %bitcast.47), channel_id=1, source_target_pairs={{31,0},{0,1},{1,2},{2,3},{3,4},{4,5},{5,6},{6,7},{7,8},{8,9},{9,10... | collective-permute-start | bytes 393224 | tf_op jit(solution)/shard_map/ppermute | solution.py:11
  267.6 8.6 %collective-permute-start.7 = (bf16[256,256]{1,0:T(8,128)(2,1)S(1)}, bf16[256,256]{1,0:T(8,128)(2,1)S(1)}, u32[]{:S(2)}, u32[]{:S(2)}) collective-permute-start(bf16[256,256]{1,0:T(8,128)(2,1)S(1)} %broadcast_select_fusion.6), channel_id=1, source_target_pairs={{30,0},{31,1},{0,2},{1,3},{2,4},{3,5},{4,6},{5,7},{6,8},{7,9},{8,1... | collective-permute-start | bytes 393224 | tf_op jit(solution)/shard_map/ppermute | solution.py:11
  276.3 9.1 %collective-permute-start.8 = (bf16[256,256]{1,0:T(8,128)(2,1)S(1)}, bf16[256,256]{1,0:T(8,128)(2,1)S(1)}, u32[]{:S(2)}, u32[]{:S(2)}) collective-permute-start(bf16[256,256]{1,0:T(8,128)(2,1)S(1)} %broadcast_select_fusion.9), channel_id=1, source_target_pairs={{28,0},{29,1},{30,2},{31,3},{0,4},{1,5},{2,6},{3,7},{4,8},{5,9},{6... | collective-permute-start | bytes 393224 | tf_op jit(solution)/shard_map/ppermute | solution.py:11
  277.2 8.2 %collective-permute-start.10 = (bf16[256,256]{1,0:T(8,128)(2,1)S(1)}, bf16[256,256]{1,0:T(8,128)(2,1)S(1)}, u32[]{:S(2)}, u32[]{:S(2)}) collective-permute-start(bf16[256,256]{1,0:T(8,128)(2,1)S(1)} %bitcast.48), channel_id=1, source_target_pairs={{31,0},{0,1},{1,2},{2,3},{3,4},{4,5},{5,6},{6,7},{7,8},{8,9},{9,10... | collective-permute-start | bytes 393224 | tf_op jit(solution)/shard_map/ppermute | solution.py:11
  277.3 26.7 %collective-permute-start.5 = (bf16[256,2048]{1,0:T(8,128)(2,1)S(1)}, bf16[256,2048]{1,0:T(8,128)(2,1)S(1)}, u32[]{:S(2)}, u32[]{:S(2)}) collective-permute-start(bf16[256,2048]{1,0:T(8,128)(2,1)S(1)} %collective-permute-done.4), channel_id=1, source_target_pairs={{1,0},{2,1},{3,2},{4,3},{5,4},{6,5},{7,6},{8,7},{9,8},{10,9},{11,1... | collective-permute-start | bytes 3145736 | tf_op jit(solution)/shard_map/ppermute | solution.py:11
  285.4 8.1 %collective-permute-start.11 = (bf16[256,256]{1,0:T(8,128)(2,1)S(1)}, bf16[256,256]{1,0:T(8,128)(2,1)S(1)}, u32[]{:S(2)}, u32[]{:S(2)}) collective-permute-start(bf16[256,256]{1,0:T(8,128)(2,1)S(1)} %collective-permute-done.10), channel_id=1, source_target_pairs={{31,0},{0,1},{1,2},{2,3},{3,4},{4,5},{5,6},{6,7},{7,8},{8,9},{9,10... | collective-permute-start | bytes 393224 | tf_op jit(solution)/shard_map/ppermute | solution.py:11
  285.4 12.9 %collective-permute-start.9 = (bf16[256,256]{1,0:T(8,128)(2,1)S(1)}, bf16[256,256]{1,0:T(8,128)(2,1)S(1)}, u32[]{:S(2)}, u32[]{:S(2)}) collective-permute-start(bf16[256,256]{1,0:T(8,128)(2,1)S(1)} %broadcast_select_fusion.12), channel_id=1, source_target_pairs={{24,0},{25,1},{26,2},{27,3},{28,4},{29,5},{30,6},{31,7},{0,8},{1,9... | collective-permute-start | bytes 393224 | tf_op jit(solution)/shard_map/ppermute | solution.py:11
  293.5 10.4 %collective-permute-start.12 = (bf16[256,256]{1,0:T(8,128)(2,1)S(1)}, bf16[256,256]{1,0:T(8,128)(2,1)S(1)}, u32[]{:S(2)}, u32[]{:S(2)}) collective-permute-start(bf16[256,256]{1,0:T(8,128)(2,1)S(1)} %broadcast_select_fusion.5), channel_id=1, source_target_pairs={{30,0},{31,1},{0,2},{1,3},{2,4},{3,5},{4,6},{5,7},{6,8},{7,9},{8,1... | collective-permute-start | bytes 393224 | tf_op jit(solution)/shard_map/ppermute | solution.py:11
  303.9 7.8 %collective-permute-start.13 = (bf16[256,256]{1,0:T(8,128)(2,1)S(1)}, bf16[256,256]{1,0:T(8,128)(2,1)S(1)}, u32[]{:S(2)}, u32[]{:S(2)}) collective-permute-start(bf16[256,256]{1,0:T(8,128)(2,1)S(1)} %broadcast_select_fusion.8), channel_id=1, source_target_pairs={{28,0},{29,1},{30,2},{31,3},{0,4},{1,5},{2,6},{3,7},{4,8},{5,9},{6... | collective-permute-start | bytes 393224 | tf_op jit(solution)/shard_map/ppermute | solution.py:11
  304.8 9.4 %collective-permute-start.15 = (bf16[256,256]{1,0:T(8,128)(2,1)S(1)}, bf16[256,256]{1,0:T(8,128)(2,1)S(1)}, u32[]{:S(2)}, u32[]{:S(2)}) collective-permute-start(bf16[256,256]{1,0:T(8,128)(2,1)S(1)} %bitcast.49), channel_id=1, source_target_pairs={{31,0},{0,1},{1,2},{2,3},{3,4},{4,5},{5,6},{6,7},{7,8},{8,9},{9,10... | collective-permute-start | bytes 393224 | tf_op jit(solution)/shard_map/ppermute | solution.py:11
  311.7 10.6 %collective-permute-start.14 = (bf16[256,256]{1,0:T(8,128)(2,1)S(1)}, bf16[256,256]{1,0:T(8,128)(2,1)S(1)}, u32[]{:S(2)}, u32[]{:S(2)}) collective-permute-start(bf16[256,256]{1,0:T(8,128)(2,1)S(1)} %broadcast_select_fusion.11), channel_id=1, source_target_pairs={{24,0},{25,1},{26,2},{27,3},{28,4},{29,5},{30,6},{31,7},{0,8},{1,9... | collective-permute-start | bytes 393224 | tf_op jit(solution)/shard_map/ppermute | solution.py:11
  314.2 8.0 %collective-permute-start.16 = (bf16[256,256]{1,0:T(8,128)(2,1)S(1)}, bf16[256,256]{1,0:T(8,128)(2,1)S(1)}, u32[]{:S(2)}, u32[]{:S(2)}) collective-permute-start(bf16[256,256]{1,0:T(8,128)(2,1)S(1)} %collective-permute-done.15), channel_id=1, source_target_pairs={{31,0},{0,1},{1,2},{2,3},{3,4},{4,5},{5,6},{6,7},{7,8},{8,9},{9,10... | collective-permute-start | bytes 393224 | tf_op jit(solution)/shard_map/ppermute | solution.py:11
  322.2 8.0 %collective-permute-start.17 = (bf16[256,256]{1,0:T(8,128)(2,1)S(1)}, bf16[256,256]{1,0:T(8,128)(2,1)S(1)}, u32[]{:S(2)}, u32[]{:S(2)}) collective-permute-start(bf16[256,256]{1,0:T(8,128)(2,1)S(1)} %collective-permute-done.16), channel_id=1, source_target_pairs={{31,0},{0,1},{1,2},{2,3},{3,4},{4,5},{5,6},{6,7},{7,8},{8,9},{9,10... | collective-permute-start | bytes 393224 | tf_op jit(solution)/shard_map/ppermute | solution.py:11
  330.2 10.0 %collective-permute-start.18 = (bf16[256,256]{1,0:T(8,128)(2,1)S(1)}, bf16[256,256]{1,0:T(8,128)(2,1)S(1)}, u32[]{:S(2)}, u32[]{:S(2)}) collective-permute-start(bf16[256,256]{1,0:T(8,128)(2,1)S(1)} %broadcast_select_fusion.4), channel_id=1, source_target_pairs={{30,0},{31,1},{0,2},{1,3},{2,4},{3,5},{4,6},{5,7},{6,8},{7,9},{8,1... | collective-permute-start | bytes 393224 | tf_op jit(solution)/shard_map/ppermute | solution.py:11
  340.3 7.7 %collective-permute-start.19 = (bf16[256,256]{1,0:T(8,128)(2,1)S(1)}, bf16[256,256]{1,0:T(8,128)(2,1)S(1)}, u32[]{:S(2)}, u32[]{:S(2)}) collective-permute-start(bf16[256,256]{1,0:T(8,128)(2,1)S(1)} %broadcast_select_fusion.7), channel_id=1, source_target_pairs={{28,0},{29,1},{30,2},{31,3},{0,4},{1,5},{2,6},{3,7},{4,8},{5,9},{6... | collective-permute-start | bytes 393224 | tf_op jit(solution)/shard_map/ppermute | solution.py:11
  348.0 6.8 %collective-permute-start.20 = (bf16[256,256]{1,0:T(8,128)(2,1)S(1)}, bf16[256,256]{1,0:T(8,128)(2,1)S(1)}, u32[]{:S(2)}, u32[]{:S(2)}) collective-permute-start(bf16[256,256]{1,0:T(8,128)(2,1)S(1)} %broadcast_select_fusion.10), channel_id=1, source_target_pairs={{24,0},{25,1},{26,2},{27,3},{28,4},{29,5},{30,6},{31,7},{0,8},{1,9... | collective-permute-start | bytes 393224 | tf_op jit(solution)/shard_map/ppermute | solution.py:11
Sparse Core Ops, SparseCore 0:
  13.8 131.7 all-reduce.1
where the time goes:
time: 363 us
  waiting for transfers between devices  301 us (83%)
  starting transfers between devices  18.4 us (5%)
  other arithmetic  18.1 us (5%)
  between operations  15 us (4%)
  matrix products  9.2 us (3%)
    ppermute x21, waiting for transfers between devices, shifted(): return lax.ppermute(block, axis, route)  166 us
    psum x1, waiting for transfers between devices, shards(): lax.psum(jnp.dot(picker, samples, preferred_element_type=jnp.float32), 'b...  135 us
    ppermute x21, starting transfers between devices, shifted(): return lax.ppermute(block, axis, route)  18.3 us
  transfers between devices with their start and end apart: 22, of which 18 were waited for; matrix products, arithmetic and copies ran while one was open for 2% of the time, Pallas kernels for 0%

commit v1 on v0

--- a/solution.py
+++ b/solution.py
@@ -41,7 +41,9 @@
     picker = jnp.logical_and(
         (owner == mine)[:, None], within[:, None] == jnp.arange(rows, dtype=jnp.int32)[None, :]
     ).astype(jnp.bfloat16)
-    hub_rows = lax.psum(jnp.dot(picker, samples, preferred_element_type=jnp.float32), "blk")
+    hub_rows = jnp.sum(
+        lax.all_gather(jnp.dot(picker, samples, preferred_element_type=jnp.float32), "blk"), axis=0
+    )
     gram = jnp.dot(hub_rows, hub_rows.T, precision=lax.Precision.HIGHEST)
     proj = jnp.dot(samples, hub_rows.astype(jnp.bfloat16).T, preferred_element_type=jnp.float32)
     factor_lower = jnp.linalg.cholesky(gram)

time: 363 us -> 352 us (0.970)
  waiting for transfers between devices: 301 us -> 284 us
  other arithmetic: 18.1 us -> 25.1 us
    psum x1 -> x0, waiting for transfers between devices: 135 us -> none  [shards(): lax.psum(jnp.dot(picker, samples, preferred_element_type=jnp.float32), 'b...]
    all_gather x0 -> x1, waiting for transfers between devices: none -> 118 us  [shards(): lax.all_gather(jnp.dot(picker, samples, preferred_element_type=jnp.float3...]
    reduce_sum x0 -> x1, other arithmetic: none -> 6.98 us  [shards(): jnp.sum(lax.all_gather(jnp.dot(picker, samples, preferred_element_type=jn...]
where the time goes in v1:
time: 352 us
  waiting for transfers between devices  284 us (81%)
  other arithmetic  25.1 us (7%)
  starting transfers between devices  18.6 us (5%)
  between operations  15 us (4%)
  matrix products  7.95 us (2%)
    ppermute x21, waiting for transfers between devices, shifted(): return lax.ppermute(block, axis, route)  166 us
    all_gather x1, waiting for transfers between devices, shards(): lax.all_gather(jnp.dot(picker, samples, preferred_element_type=jnp.float3...  118 us
    ppermute x21, starting transfers between devices, shifted(): return lax.ppermute(block, axis, route)  18.6 us
  transfers between devices with their start and end apart: 22, of which 18 were waited for; matrix products, arithmetic and copies ran while one was open for 2% of the time, Pallas kernels for 0%

profile of v1, /device:TPU:0, one launch (start us, length us, event | category | flops | bytes accessed | tf_op | source)
XLA Modules:
  0.0 351.6 jit_solution(9919794990849196693)
XLA Ops:
  7.2 0.7 and_select_fusion
  7.9 0.7 fusion.50
  8.5 2.4 fusion.40
  10.9 117.6 %all-gather.3.cloned.1.call-done = f32[2048,2048]{1,0:T(8,128)} async-done(((f32[64,2048]{1,0:T(8,128)}), f32[2048,2048]{1,0:T(8,128)}) %all-gather.3.cloned.1.call-update) | async-done | bytes 16777232 | tf_op jit(solution)/shard_map/all_gather | solution.py:45
  128.5 7.0 %reduce_sum.49 = f32[64,2048]{1,0:T(8,128)S(1)} reduce(f32[32,64,2048]{2,1,0:T(8,128)} %bitcast.48, f32[]{:T(128)} %constant.97.clone.1), dimensions={0}, to_apply=%region_0.1 | reduce | flops 4063232 | bytes 17301508 | tf_op jit(solution)/shard_map/reduce_sum | solution.py:44
  135.5 0.6 fusion.51
  136.0 0.4 fusion.37
  136.5 0.1 copy.6
  136.6 5.8 %cholesky.16 = f32[64,64]{1,0:T(8,128)S(1)} custom-call(f32[64,64]{1,0:T(8,128)S(1)} %fusion.47), custom_call_target="Cholesky" | custom-call | tf_op jit(solution)/shard_map/jit(cholesky)/cholesky | solution.py:49
  142.5 0.6 compare_reduce_fusion
  143.1 0.7 fusion.42
  143.8 4.9 %custom-call.10 = f32[1,64,64]{1,2,0:T(8,128)S(1)} custom-call(f32[1,64,64]{2,1,0:T(8,128)S(1)} %fusion.42), custom_call_target="InvertDiagBlocksLowerTriangular" | custom-call | tf_op jit(solution)/shard_map/jit(_cho_solve)/triangular_solve | solution.py:50
  148.7 0.3 fusion.45
  149.0 0.2 fusion.43
  149.2 2.1 multiply_reduce_fusion.3
  151.2 2.4 collective-permute-start
  154.2 11.7 %collective-permute-done = bf16[256,2048]{1,0:T(8,128)(2,1)S(1)} collective-permute-done((bf16[256,2048]{1,0:T(8,128)(2,1)S(1)}, bf16[256,2048]{1,0:T(8,128)(2,1)S(1)}, u32[]{:S(2)}, u32[]{:S(2)}) %collective-permute-start) | collective-permute-done | bytes 1048608 | tf_op jit(solution)/shard_map/ppermute | solution.py:11
  165.9 0.1 broadcast_select_fusion
  166.0 1.5 collective-permute-start.1
  167.5 23.9 %collective-permute-done.1 = bf16[256,2048]{1,0:T(8,128)(2,1)S(1)} collective-permute-done((bf16[256,2048]{1,0:T(8,128)(2,1)S(1)}, bf16[256,2048]{1,0:T(8,128)(2,1)S(1)}, u32[]{:S(2)}, u32[]{:S(2)}) %collective-permute-start.1) | collective-permute-done | bytes 1048608 | tf_op jit(solution)/shard_map/ppermute | solution.py:11
  191.4 0.1 broadcast_select_fusion.1
  191.5 0.1 collective-permute-start.2
  191.6 24.9 %collective-permute-done.2 = bf16[256,2048]{1,0:T(8,128)(2,1)S(1)} collective-permute-done((bf16[256,2048]{1,0:T(8,128)(2,1)S(1)}, bf16[256,2048]{1,0:T(8,128)(2,1)S(1)}, u32[]{:S(2)}, u32[]{:S(2)}) %collective-permute-start.2) | collective-permute-done | bytes 1048608 | tf_op jit(solution)/shard_map/ppermute | solution.py:11
  216.4 0.1 broadcast_select_fusion.2
  216.5 1.4 collective-permute-start.3
  218.0 22.6 %collective-permute-done.3 = bf16[256,2048]{1,0:T(8,128)(2,1)S(1)} collective-permute-done((bf16[256,2048]{1,0:T(8,128)(2,1)S(1)}, bf16[256,2048]{1,0:T(8,128)(2,1)S(1)}, u32[]{:S(2)}, u32[]{:S(2)}) %collective-permute-start.3) | collective-permute-done | bytes 1048608 | tf_op jit(solution)/shard_map/ppermute | solution.py:11
  240.6 0.5 multiply_reduce_fusion.2
  241.1 7.1 %collective-permute-start.4 = (bf16[256,2048]{1,0:T(8,128)(2,1)S(1)}, bf16[256,2048]{1,0:T(8,128)(2,1)S(1)}, u32[]{:S(2)}, u32[]{:S(2)}) collective-permute-start(bf16[256,2048]{1,0:T(8,128)(2,1)S(1)} %get-tuple-element.7), channel_id=1, source_target_pairs={{1,0},{2,1},{3,2},{4,3},{5,4},{6,5},{7,6},{8,7},{9,8},{10,9},{11,1... | collective-permute-start | bytes 3145736 | tf_op jit(solution)/shard_map/ppermute | solution.py:11
  248.3 0.5 fusion.6
  248.8 0.1 collective-permute-start.6
  248.8 0.5 fusion.5
  249.3 7.6 %collective-permute-done.6 = bf16[256,256]{1,0:T(8,128)(2,1)S(1)} collective-permute-done((bf16[256,256]{1,0:T(8,128)(2,1)S(1)}, bf16[256,256]{1,0:T(8,128)(2,1)S(1)}, u32[]{:S(2)}, u32[]{:S(2)}) %collective-permute-start.6) | collective-permute-done | bytes 131104 | tf_op jit(solution)/shard_map/ppermute | solution.py:11
  256.9 0.1 collective-permute-start.7
  257.0 0.9 fusion.11
  257.9 7.6 %collective-permute-done.7 = bf16[256,256]{1,0:T(8,128)(2,1)S(1)} collective-permute-done((bf16[256,256]{1,0:T(8,128)(2,1)S(1)}, bf16[256,256]{1,0:T(8,128)(2,1)S(1)}, u32[]{:S(2)}, u32[]{:S(2)}) %collective-permute-start.7) | collective-permute-done | bytes 131104 | tf_op jit(solution)/shard_map/ppermute | solution.py:11
  265.6 0.3 multiply_reduce_fusion.1
  265.9 0.6 fusion.7
  266.6 5.3 %collective-permute-start.5 = (bf16[256,2048]{1,0:T(8,128)(2,1)S(1)}, bf16[256,2048]{1,0:T(8,128)(2,1)S(1)}, u32[]{:S(2)}, u32[]{:S(2)}) collective-permute-start(bf16[256,2048]{1,0:T(8,128)(2,1)S(1)} %collective-permute-done.4), channel_id=1, source_target_pairs={{1,0},{2,1},{3,2},{4,3},{5,4},{6,5},{7,6},{8,7},{9,8},{10,9},{11,1... | collective-permute-start | bytes 3145736 | tf_op jit(solution)/shard_map/ppermute | solution.py:11
  271.9 0.2 fusion.15
  272.1 2.6 collective-permute-done.10
  274.7 0.1 collective-permute-start.9
  274.8 8.0 %collective-permute-done.11 = bf16[256,256]{1,0:T(8,128)(2,1)S(1)} collective-permute-done((bf16[256,256]{1,0:T(8,128)(2,1)S(1)}, bf16[256,256]{1,0:T(8,128)(2,1)S(1)}, u32[]{:S(2)}, u32[]{:S(2)}) %collective-permute-start.11) | collective-permute-done | bytes 131104 | tf_op jit(solution)/shard_map/ppermute | solution.py:11
  282.8 0.1 collective-permute-start.12
  282.8 4.6 %collective-permute-done.9 = bf16[256,256]{1,0:T(8,128)(2,1)S(1)} collective-permute-done((bf16[256,256]{1,0:T(8,128)(2,1)S(1)}, bf16[256,256]{1,0:T(8,128)(2,1)S(1)}, u32[]{:S(2)}, u32[]{:S(2)}) %collective-permute-start.9) | collective-permute-done | bytes 131104 | tf_op jit(solution)/shard_map/ppermute | solution.py:11
  287.5 5.4 %collective-permute-done.12 = bf16[256,256]{1,0:T(8,128)(2,1)S(1)} collective-permute-done((bf16[256,256]{1,0:T(8,128)(2,1)S(1)}, bf16[256,256]{1,0:T(8,128)(2,1)S(1)}, u32[]{:S(2)}, u32[]{:S(2)}) %collective-permute-start.12) | collective-permute-done | bytes 131104 | tf_op jit(solution)/shard_map/ppermute | solution.py:11
  292.9 0.1 collective-permute-start.13
  293.0 0.3 multiply_reduce_fusion
  293.3 0.6 fusion.8
  293.9 6.9 %collective-permute-done.13 = bf16[256,256]{1,0:T(8,128)(2,1)S(1)} collective-permute-done((bf16[256,256]{1,0:T(8,128)(2,1)S(1)}, bf16[256,256]{1,0:T(8,128)(2,1)S(1)}, u32[]{:S(2)}, u32[]{:S(2)}) %collective-permute-start.13) | collective-permute-done | bytes 131104 | tf_op jit(solution)/shard_map/ppermute | solution.py:11
  300.8 0.1 collective-permute-start.14
  300.9 2.2 collective-permute-done.15
  303.1 0.2 fusion.19
  303.3 7.8 %collective-permute-done.16 = bf16[256,256]{1,0:T(8,128)(2,1)S(1)} collective-permute-done((bf16[256,256]{1,0:T(8,128)(2,1)S(1)}, bf16[256,256]{1,0:T(8,128)(2,1)S(1)}, u32[]{:S(2)}, u32[]{:S(2)}) %collective-permute-start.16) | collective-permute-done | bytes 131104 | tf_op jit(solution)/shard_map/ppermute | solution.py:11
  311.1 8.0 %collective-permute-done.17 = bf16[256,256]{1,0:T(8,128)(2,1)S(1)} collective-permute-done((bf16[256,256]{1,0:T(8,128)(2,1)S(1)}, bf16[256,256]{1,0:T(8,128)(2,1)S(1)}, u32[]{:S(2)}, u32[]{:S(2)}) %collective-permute-start.17) | collective-permute-done | bytes 131104 | tf_op jit(solution)/shard_map/ppermute | solution.py:11
  319.1 0.1 collective-permute-start.18
  319.1 0.4 fusion.27
  319.5 9.5 %collective-permute-done.18 = bf16[256,256]{1,0:T(8,128)(2,1)S(1)} collective-permute-done((bf16[256,256]{1,0:T(8,128)(2,1)S(1)}, bf16[256,256]{1,0:T(8,128)(2,1)S(1)}, u32[]{:S(2)}, u32[]{:S(2)}) %collective-permute-start.18) | collective-permute-done | bytes 131104 | tf_op jit(solution)/shard_map/ppermute | solution.py:11
  329.1 0.2 fusion.23
  329.3 7.5 %collective-permute-done.19 = bf16[256,256]{1,0:T(8,128)(2,1)S(1)} collective-permute-done((bf16[256,256]{1,0:T(8,128)(2,1)S(1)}, bf16[256,256]{1,0:T(8,128)(2,1)S(1)}, u32[]{:S(2)}, u32[]{:S(2)}) %collective-permute-start.19) | collective-permute-done | bytes 131104 | tf_op jit(solution)/shard_map/ppermute | solution.py:11
  336.8 0.1 collective-permute-start.20
  336.9 1.1 copy.14
  338.1 5.5 %collective-permute-done.20 = bf16[256,256]{1,0:T(8,128)(2,1)S(1)} collective-permute-done((bf16[256,256]{1,0:T(8,128)(2,1)S(1)}, bf16[256,256]{1,0:T(8,128)(2,1)S(1)}, u32[]{:S(2)}, u32[]{:S(2)}) %collective-permute-start.20) | collective-permute-done | bytes 131104 | tf_op jit(solution)/shard_map/ppermute | solution.py:11
  343.6 0.2 fusion.35
  343.8 0.9 pad_maximum_fusion.1
  (34 shorter events, 0.6 us)
Async XLA Ops:
  7.2 121.3 %all-gather.3.cloned.1.call-start = ((), (), s32[]{:S(2)}) async-start(), calls=%async_computation | async-start | bytes 17301504 | tf_op jit(solution)/shard_map/all_gather | solution.py:45
  128.5 7.6 %copy-start = (bf16[256,2048]{1,0:T(8,128)(2,1)S(1)}, bf16[256,2048]{1,0:T(8,128)(2,1)}, u32[]{:S(2)}) copy-start(bf16[256,2048]{1,0:T(8,128)(2,1)} %param.3) | copy-start | bytes 3145732
  151.2 14.7 %collective-permute-start = (bf16[256,2048]{1,0:T(8,128)(2,1)S(1)}, bf16[256,2048]{1,0:T(8,128)(2,1)S(1)}, u32[]{:S(2)}, u32[]{:S(2)}) collective-permute-start(bf16[256,2048]{1,0:T(8,128)(2,1)S(1)} %get-tuple-element.9), channel_id=1, source_target_pairs={{1,0},{2,1},{3,2},{4,3},{5,4},{6,5},{7,6},{8,7},{9,8},{10,9},{11,1... | collective-permute-start | bytes 3145736 | tf_op jit(solution)/shard_map/ppermute | solution.py:11
  166.0 25.4 %collective-permute-start.1 = (bf16[256,2048]{1,0:T(8,128)(2,1)S(1)}, bf16[256,2048]{1,0:T(8,128)(2,1)S(1)}, u32[]{:S(2)}, u32[]{:S(2)}) collective-permute-start(bf16[256,2048]{1,0:T(8,128)(2,1)S(1)} %broadcast_select_fusion), channel_id=1, source_target_pairs={{2,0},{3,1},{4,2},{5,3},{6,4},{7,5},{8,6},{9,7},{10,8},{11,9},{12,... | collective-permute-start | bytes 3145736 | tf_op jit(solution)/shard_map/ppermute | solution.py:11
  191.5 24.9 %collective-permute-start.2 = (bf16[256,2048]{1,0:T(8,128)(2,1)S(1)}, bf16[256,2048]{1,0:T(8,128)(2,1)S(1)}, u32[]{:S(2)}, u32[]{:S(2)}) collective-permute-start(bf16[256,2048]{1,0:T(8,128)(2,1)S(1)} %broadcast_select_fusion.1), channel_id=1, source_target_pairs={{4,0},{5,1},{6,2},{7,3},{8,4},{9,5},{10,6},{11,7},{12,8},{13,9},{1... | collective-permute-start | bytes 3145736 | tf_op jit(solution)/shard_map/ppermute | solution.py:11
  216.5 24.1 %collective-permute-start.3 = (bf16[256,2048]{1,0:T(8,128)(2,1)S(1)}, bf16[256,2048]{1,0:T(8,128)(2,1)S(1)}, u32[]{:S(2)}, u32[]{:S(2)}) collective-permute-start(bf16[256,2048]{1,0:T(8,128)(2,1)S(1)} %broadcast_select_fusion.2), channel_id=1, source_target_pairs={{8,0},{9,1},{10,2},{11,3},{12,4},{13,5},{14,6},{15,7},{16,8},{17,9... | collective-permute-start | bytes 3145736 | tf_op jit(solution)/shard_map/ppermute | solution.py:11
  241.1 24.5 %collective-permute-start.4 = (bf16[256,2048]{1,0:T(8,128)(2,1)S(1)}, bf16[256,2048]{1,0:T(8,128)(2,1)S(1)}, u32[]{:S(2)}, u32[]{:S(2)}) collective-permute-start(bf16[256,2048]{1,0:T(8,128)(2,1)S(1)} %get-tuple-element.7), channel_id=1, source_target_pairs={{1,0},{2,1},{3,2},{4,3},{5,4},{6,5},{7,6},{8,7},{9,8},{10,9},{11,1... | collective-permute-start | bytes 3145736 | tf_op jit(solution)/shard_map/ppermute | solution.py:11
  248.8 8.1 %collective-permute-start.6 = (bf16[256,256]{1,0:T(8,128)(2,1)S(1)}, bf16[256,256]{1,0:T(8,128)(2,1)S(1)}, u32[]{:S(2)}, u32[]{:S(2)}) collective-permute-start(bf16[256,256]{1,0:T(8,128)(2,1)S(1)} %bitcast.49), channel_id=1, source_target_pairs={{31,0},{0,1},{1,2},{2,3},{3,4},{4,5},{5,6},{6,7},{7,8},{8,9},{9,10... | collective-permute-start | bytes 393224 | tf_op jit(solution)/shard_map/ppermute | solution.py:11
  256.9 8.6 %collective-permute-start.7 = (bf16[256,256]{1,0:T(8,128)(2,1)S(1)}, bf16[256,256]{1,0:T(8,128)(2,1)S(1)}, u32[]{:S(2)}, u32[]{:S(2)}) collective-permute-start(bf16[256,256]{1,0:T(8,128)(2,1)S(1)} %broadcast_select_fusion.6), channel_id=1, source_target_pairs={{30,0},{31,1},{0,2},{1,3},{2,4},{3,5},{4,6},{5,7},{6,8},{7,9},{8,1... | collective-permute-start | bytes 393224 | tf_op jit(solution)/shard_map/ppermute | solution.py:11
  265.6 9.1 %collective-permute-start.8 = (bf16[256,256]{1,0:T(8,128)(2,1)S(1)}, bf16[256,256]{1,0:T(8,128)(2,1)S(1)}, u32[]{:S(2)}, u32[]{:S(2)}) collective-permute-start(bf16[256,256]{1,0:T(8,128)(2,1)S(1)} %broadcast_select_fusion.9), channel_id=1, source_target_pairs={{28,0},{29,1},{30,2},{31,3},{0,4},{1,5},{2,6},{3,7},{4,8},{5,9},{6... | collective-permute-start | bytes 393224 | tf_op jit(solution)/shard_map/ppermute | solution.py:11
  266.5 8.2 %collective-permute-start.10 = (bf16[256,256]{1,0:T(8,128)(2,1)S(1)}, bf16[256,256]{1,0:T(8,128)(2,1)S(1)}, u32[]{:S(2)}, u32[]{:S(2)}) collective-permute-start(bf16[256,256]{1,0:T(8,128)(2,1)S(1)} %bitcast.50), channel_id=1, source_target_pairs={{31,0},{0,1},{1,2},{2,3},{3,4},{4,5},{5,6},{6,7},{7,8},{8,9},{9,10... | collective-permute-start | bytes 393224 | tf_op jit(solution)/shard_map/ppermute | solution.py:11
  266.6 26.4 %collective-permute-start.5 = (bf16[256,2048]{1,0:T(8,128)(2,1)S(1)}, bf16[256,2048]{1,0:T(8,128)(2,1)S(1)}, u32[]{:S(2)}, u32[]{:S(2)}) collective-permute-start(bf16[256,2048]{1,0:T(8,128)(2,1)S(1)} %collective-permute-done.4), channel_id=1, source_target_pairs={{1,0},{2,1},{3,2},{4,3},{5,4},{6,5},{7,6},{8,7},{9,8},{10,9},{11,1... | collective-permute-start | bytes 3145736 | tf_op jit(solution)/shard_map/ppermute | solution.py:11
  274.7 8.1 %collective-permute-start.11 = (bf16[256,256]{1,0:T(8,128)(2,1)S(1)}, bf16[256,256]{1,0:T(8,128)(2,1)S(1)}, u32[]{:S(2)}, u32[]{:S(2)}) collective-permute-start(bf16[256,256]{1,0:T(8,128)(2,1)S(1)} %collective-permute-done.10), channel_id=1, source_target_pairs={{31,0},{0,1},{1,2},{2,3},{3,4},{4,5},{5,6},{6,7},{7,8},{8,9},{9,10... | collective-permute-start | bytes 393224 | tf_op jit(solution)/shard_map/ppermute | solution.py:11
  274.7 12.8 %collective-permute-start.9 = (bf16[256,256]{1,0:T(8,128)(2,1)S(1)}, bf16[256,256]{1,0:T(8,128)(2,1)S(1)}, u32[]{:S(2)}, u32[]{:S(2)}) collective-permute-start(bf16[256,256]{1,0:T(8,128)(2,1)S(1)} %broadcast_select_fusion.12), channel_id=1, source_target_pairs={{24,0},{25,1},{26,2},{27,3},{28,4},{29,5},{30,6},{31,7},{0,8},{1,9... | collective-permute-start | bytes 393224 | tf_op jit(solution)/shard_map/ppermute | solution.py:11
  282.8 10.1 %collective-permute-start.12 = (bf16[256,256]{1,0:T(8,128)(2,1)S(1)}, bf16[256,256]{1,0:T(8,128)(2,1)S(1)}, u32[]{:S(2)}, u32[]{:S(2)}) collective-permute-start(bf16[256,256]{1,0:T(8,128)(2,1)S(1)} %broadcast_select_fusion.5), channel_id=1, source_target_pairs={{30,0},{31,1},{0,2},{1,3},{2,4},{3,5},{4,6},{5,7},{6,8},{7,9},{8,1... | collective-permute-start | bytes 393224 | tf_op jit(solution)/shard_map/ppermute | solution.py:11
  292.9 7.9 %collective-permute-start.13 = (bf16[256,256]{1,0:T(8,128)(2,1)S(1)}, bf16[256,256]{1,0:T(8,128)(2,1)S(1)}, u32[]{:S(2)}, u32[]{:S(2)}) collective-permute-start(bf16[256,256]{1,0:T(8,128)(2,1)S(1)} %broadcast_select_fusion.8), channel_id=1, source_target_pairs={{28,0},{29,1},{30,2},{31,3},{0,4},{1,5},{2,6},{3,7},{4,8},{5,9},{6... | collective-permute-start | bytes 393224 | tf_op jit(solution)/shard_map/ppermute | solution.py:11
  293.9 9.2 %collective-permute-start.15 = (bf16[256,256]{1,0:T(8,128)(2,1)S(1)}, bf16[256,256]{1,0:T(8,128)(2,1)S(1)}, u32[]{:S(2)}, u32[]{:S(2)}) collective-permute-start(bf16[256,256]{1,0:T(8,128)(2,1)S(1)} %bitcast.51), channel_id=1, source_target_pairs={{31,0},{0,1},{1,2},{2,3},{3,4},{4,5},{5,6},{6,7},{7,8},{8,9},{9,10... | collective-permute-start | bytes 393224 | tf_op jit(solution)/shard_map/ppermute | solution.py:11
  300.8 10.3 %collective-permute-start.14 = (bf16[256,256]{1,0:T(8,128)(2,1)S(1)}, bf16[256,256]{1,0:T(8,128)(2,1)S(1)}, u32[]{:S(2)}, u32[]{:S(2)}) collective-permute-start(bf16[256,256]{1,0:T(8,128)(2,1)S(1)} %broadcast_select_fusion.11), channel_id=1, source_target_pairs={{24,0},{25,1},{26,2},{27,3},{28,4},{29,5},{30,6},{31,7},{0,8},{1,9... | collective-permute-start | bytes 393224 | tf_op jit(solution)/shard_map/ppermute | solution.py:11
  303.1 8.0 %collective-permute-start.16 = (bf16[256,256]{1,0:T(8,128)(2,1)S(1)}, bf16[256,256]{1,0:T(8,128)(2,1)S(1)}, u32[]{:S(2)}, u32[]{:S(2)}) collective-permute-start(bf16[256,256]{1,0:T(8,128)(2,1)S(1)} %collective-permute-done.15), channel_id=1, source_target_pairs={{31,0},{0,1},{1,2},{2,3},{3,4},{4,5},{5,6},{6,7},{7,8},{8,9},{9,10... | collective-permute-start | bytes 393224 | tf_op jit(solution)/shard_map/ppermute | solution.py:11
  311.1 8.0 %collective-permute-start.17 = (bf16[256,256]{1,0:T(8,128)(2,1)S(1)}, bf16[256,256]{1,0:T(8,128)(2,1)S(1)}, u32[]{:S(2)}, u32[]{:S(2)}) collective-permute-start(bf16[256,256]{1,0:T(8,128)(2,1)S(1)} %collective-permute-done.16), channel_id=1, source_target_pairs={{31,0},{0,1},{1,2},{2,3},{3,4},{4,5},{5,6},{6,7},{7,8},{8,9},{9,10... | collective-permute-start | bytes 393224 | tf_op jit(solution)/shard_map/ppermute | solution.py:11
  319.1 10.0 %collective-permute-start.18 = (bf16[256,256]{1,0:T(8,128)(2,1)S(1)}, bf16[256,256]{1,0:T(8,128)(2,1)S(1)}, u32[]{:S(2)}, u32[]{:S(2)}) collective-permute-start(bf16[256,256]{1,0:T(8,128)(2,1)S(1)} %broadcast_select_fusion.4), channel_id=1, source_target_pairs={{30,0},{31,1},{0,2},{1,3},{2,4},{3,5},{4,6},{5,7},{6,8},{7,9},{8,1... | collective-permute-start | bytes 393224 | tf_op jit(solution)/shard_map/ppermute | solution.py:11
  329.1 7.7 %collective-permute-start.19 = (bf16[256,256]{1,0:T(8,128)(2,1)S(1)}, bf16[256,256]{1,0:T(8,128)(2,1)S(1)}, u32[]{:S(2)}, u32[]{:S(2)}) collective-permute-start(bf16[256,256]{1,0:T(8,128)(2,1)S(1)} %broadcast_select_fusion.7), channel_id=1, source_target_pairs={{28,0},{29,1},{30,2},{31,3},{0,4},{1,5},{2,6},{3,7},{4,8},{5,9},{6... | collective-permute-start | bytes 393224 | tf_op jit(solution)/shard_map/ppermute | solution.py:11
  336.8 6.8 %collective-permute-start.20 = (bf16[256,256]{1,0:T(8,128)(2,1)S(1)}, bf16[256,256]{1,0:T(8,128)(2,1)S(1)}, u32[]{:S(2)}, u32[]{:S(2)}) collective-permute-start(bf16[256,256]{1,0:T(8,128)(2,1)S(1)} %broadcast_select_fusion.10), channel_id=1, source_target_pairs={{24,0},{25,1},{26,2},{27,3},{28,4},{29,5},{30,6},{31,7},{0,8},{1,9... | collective-permute-start | bytes 393224 | tf_op jit(solution)/shard_map/ppermute | solution.py:11
Sparse Core Ops, SparseCore 0:
  11.4 117.0 all-gather.2
